TPU v7x, 512 devices: a whole 4x8x8 slice. The times are simulated.
512 devices in a mesh: seq: 16 (over y, core), exp: 32 (over x, z).
Axes of the slice: x: 4, y: 8, z: 8, core: 2. Of those that a mesh axis runs over, the one named last changes fastest.
Arguments:
- tokens: bfloat16 [65536, 1280], P(('seq', 'exp')), may hold values from -64 to 64
- slot_keys: bfloat16 [1280, 32], P(None, 'exp'), may hold values from -3 to 3
- w_in: bfloat16 [32, 5120, 1280], P('exp', 'seq'), may hold values from -0.15625 to 0.15625
- w_out: bfloat16 [32, 5120, 1280], P('exp', 'seq'), may hold values from -0.078125 to 0.078125
- cotangent: bfloat16 [65536, 1280], P(('seq', 'exp')), may hold values from -6 to 6
Outputs:
- layer_out: bfloat16 [65536, 1280], P(('seq', 'exp'))
- tokens_grad: bfloat16 [65536, 1280], P(('seq', 'exp'))
- keys_grad: float32 [1280, 32], P(None, 'exp')
- w_in_grad: bfloat16 [32, 5120, 1280], P('exp', 'seq')
- w_out_grad: bfloat16 [32, 5120, 1280], P('exp', 'seq')
All inputs are finite; a program needn't handle non-finite values.
Results may differ from a plain program's by a relative error of at most 0.03.
Values may be sent and summed in bfloat16 or wider, within the bound.
A program may use at most 64 MiB of HBM per device.

v0:
```python
import jax
import jax.numpy as jnp
from jax import lax
from jax.sharding import Mesh
from jax.sharding import PartitionSpec as P

EXP = ("exp_0", "exp_1")
SEQ = ("seq_0", "seq_1")
SEQ_EXP = ("seq_0", "seq_1", "exp_0", "exp_1")


tanh_coeff = 0.7978845608028654
cubic_coeff = 0.044715


def cut_along(value, dim, size):
    before, after = (value.shape[:dim], value.shape[dim + 1 :])
    return jnp.moveaxis(value.reshape(*before, size, -1, *after), dim, 0)


def sent_and_summed(value, axis, dim):
    tiles = cut_along(value, dim, lax.axis_size(axis))
    arrived = lax.all_to_all(tiles, axis, split_axis=0, concat_axis=0, tiled=True)
    return arrived.sum(axis=0)


def sent_to_all(value, axis):
    copies = jnp.broadcast_to(value, (lax.axis_size(axis), *value.shape))
    return lax.all_to_all(copies, axis, split_axis=0, concat_axis=0, tiled=True)


def taken_together(value, axis):
    return sent_to_all(value, axis).sum(axis=0)


def laid_out(tiles, dim):
    tiles = jnp.moveaxis(tiles, 0, dim)
    lengths = tiles.shape
    return tiles.reshape(*lengths[:dim], lengths[dim] * lengths[dim + 1], *lengths[dim + 2 :])


def gathered_copies(value, axis, dim):
    return laid_out(sent_to_all(value, axis), dim)


def collected_together(value, axis):
    leaves = jax.tree.leaves(value)
    sequence = sorted(range(len(leaves)), key=lambda k: -leaves[k].size)
    width = (1, *leaves[sequence[0]].shape)[-1]
    lines = [
        jnp.pad(leaves[k].reshape(-1), (0, -leaves[k].size % width)).reshape(-1, width)
        for k in sequence
    ]
    both, at, found = (lax.all_gather(jnp.concatenate(lines), axis), 0, {})
    for k, line in zip(sequence, lines):
        slab = both[:, at : at + len(line)].reshape(len(both), -1)
        found[k] = slab[:, : leaves[k].size].reshape(-1, *leaves[k].shape)
        at += len(line)
    numbers = iter(range(len(leaves)))
    return jax.tree.map(lambda _: found[next(numbers)], value)


def merged_by_axis(value, axes, combine):
    for axis in axes:
        pieces = collected_together(value, axis)
        value = jax.tree.map(lambda part: part[0], pieces)
        for k in range(1, lax.axis_size(axis)):
            value = combine(value, jax.tree.map(lambda part: part[k], pieces))
    return value


def by_axis(value, axes):
    for axis in axes:
        value = lax.psum(value, axis)
    return value


def gelu_value(values):
    return (
        0.5
        * values
        * (1.0 + jnp.tanh(tanh_coeff * (values + cubic_coeff * values * values * values)))
    )


def gelu_slope(values):
    tanh_part = jnp.tanh(tanh_coeff * (values + cubic_coeff * values * values * values))
    return 0.5 * (1.0 + tanh_part) + 0.5 * values * (1.0 - tanh_part * tanh_part) * tanh_coeff * (
        1.0 + 3.0 * cubic_coeff * values * values
    )


def join_stats(earlier, later):
    top_score = jnp.maximum(earlier[0], later[0])
    summed = earlier[1] * jnp.exp(earlier[0] - top_score) + later[1] * jnp.exp(later[0] - top_score)
    return (top_score, summed)


def rows_of(weights, row_data):

    def make_rows(first_row, row_count):
        return jnp.dot(weights, row_data, preferred_element_type=jnp.float32)

    return make_rows


def rows_paired(first_weights, first_data, second_weights, second_data):

    def make_rows(first_row, row_count):
        return jnp.concatenate(
            [
                jnp.dot(first_weights, first_data, preferred_element_type=jnp.float32),
                jnp.dot(second_weights, second_data, preferred_element_type=jnp.float32),
            ],
            axis=1,
        )

    return make_rows


def to_owners(make_rows, local_experts):
    owned_rows = sent_and_summed(
        make_rows(jnp.int32(0), local_experts * lax.axis_size(EXP)), EXP, 0
    )
    result = taken_together(owned_rows, SEQ)
    return result


def to_tokens(partial_value):
    summed = taken_together(partial_value, SEQ)
    return gathered_copies(summed.astype(jnp.bfloat16), EXP, 0)


def local(tokens, slot_keys, w_in, w_out, cotangent):
    local_experts = w_in.shape[0]
    width = tokens.shape[1]
    keys_all = gathered_copies(slot_keys, EXP, 1)
    logits = lax.dot_general(
        keys_all, tokens, (((0,), (1,)), ((), ())), preferred_element_type=jnp.float32
    )
    local_peak = jnp.max(logits, axis=1)
    local_total = jnp.sum(jnp.exp(logits - local_peak[:, None]), axis=1)
    slot_peak, slot_total = merged_by_axis((local_peak, local_total), SEQ_EXP, join_stats)
    exp_terms = jnp.exp(logits - slot_peak[:, None])
    disp_prob = exp_terms / slot_total[:, None]
    dispatch = disp_prob.astype(jnp.bfloat16)
    row_peak = jnp.max(logits, axis=0, keepdims=True)
    row_terms = jnp.exp(logits - row_peak)
    comb_prob = row_terms / jnp.sum(row_terms, axis=0, keepdims=True)
    combine = comb_prob.astype(jnp.bfloat16)
    both_rows = to_owners(rows_paired(dispatch, tokens, combine, cotangent), local_experts).astype(
        jnp.bfloat16
    )
    slot_in = both_rows[:, :width]
    early_grad = both_rows[:, width:]
    pre_act = jnp.einsum("efd,ed->ef", w_in, slot_in, preferred_element_type=jnp.float32)
    activation = gelu_value(pre_act).astype(jnp.bfloat16)
    slot_out = to_tokens(
        jnp.einsum("ef,efd->ed", activation, w_out, preferred_element_type=jnp.float32)
    )
    layer_out = lax.dot_general(
        combine, slot_out, (((0,), (0,)), ((), ())), preferred_element_type=jnp.float32
    ).astype(jnp.bfloat16)
    comb_grad = lax.dot_general(
        slot_out, cotangent, (((1,), (1,)), ((), ())), preferred_element_type=jnp.float32
    )
    act_grad = jnp.einsum("efd,ed->ef", w_out, early_grad, preferred_element_type=jnp.float32)
    w_out_grad = (
        activation.astype(jnp.float32)[:, :, None] * early_grad.astype(jnp.float32)[:, None, :]
    ).astype(jnp.bfloat16)
    pre_grad = (act_grad * gelu_slope(pre_act)).astype(jnp.bfloat16)
    w_in_grad = (
        pre_grad.astype(jnp.float32)[:, :, None] * slot_in.astype(jnp.float32)[:, None, :]
    ).astype(jnp.bfloat16)
    slot_in_grad = to_tokens(
        jnp.einsum("ef,efd->ed", pre_grad, w_in, preferred_element_type=jnp.float32)
    )
    disp_grad = lax.dot_general(
        slot_in_grad, tokens, (((1,), (1,)), ((), ())), preferred_element_type=jnp.float32
    )
    correction = by_axis(jnp.sum(disp_prob * disp_grad, axis=1), SEQ_EXP)
    comb_mean = jnp.sum(comb_prob * comb_grad, axis=0, keepdims=True)
    logit_grad = (
        comb_prob * (comb_grad - comb_mean) + disp_prob * (disp_grad - correction[:, None])
    ).astype(jnp.bfloat16)
    tokens_grad = (
        lax.dot_general(
            dispatch, slot_in_grad, (((0,), (0,)), ((), ())), preferred_element_type=jnp.float32
        )
        + lax.dot_general(
            logit_grad, keys_all, (((0,), (1,)), ((), ())), preferred_element_type=jnp.float32
        )
    ).astype(jnp.bfloat16)
    keys_rows = to_owners(rows_of(logit_grad, tokens), local_experts)
    keys_grad = keys_rows.T
    return (layer_out, tokens_grad, keys_grad, w_in_grad, w_out_grad)


def solution(mesh):
    finer = Mesh(mesh.devices.reshape(8, 2, 4, 8), ("seq_0", "seq_1", "exp_0", "exp_1"))
    placed = (
        P(SEQ_EXP, None),
        P(None, EXP),
        P(EXP, SEQ, None),
        P(EXP, SEQ, None),
        P(SEQ_EXP, None),
    )
    return jax.shard_map(
        local,
        mesh=finer,
        in_specs=placed,
        out_specs=(
            P(SEQ_EXP, None),
            P(SEQ_EXP, None),
            P(None, EXP),
            P(EXP, SEQ, None),
            P(EXP, SEQ, None),
        ),
        check_vma=False,
    )
```

profile of v0, /device:TPU:1, one launch (start us, length us, event | category | flops | bytes accessed | tf_op | source)
XLA Modules:
  0.0 225.8 jit_solution(24418915979443625)
XLA Ops:
  0.7 0.8 reduce.6
  1.6 0.5 broadcast.144
  2.1 1.1 reduce.19
  3.2 22.6 %all_to_all.45 = bf16[32,2,640]{2,1,0:T(2,128)(2,1)S(1)} all-to-all(bf16[32,2,640]{2,1,0:T(2,128)(2,1)S(1)} %reshape.1141), channel_id=1, replica_groups=mesh['seq_0'=8,'seq_1'=2,'exp_0'=4,'exp_1'=8] {'exp_0','exp_1'}, dimensions={0} | all-to-all | bytes 163840 | tf_op jit(solution)/shard_map/all_to_all | solution.py:29
  25.9 0.3 fusion.114
  26.4 13.3 %all-gather.4 = f32[8,2,32]{2,1,0:T(2,128)S(1)} all-gather(f32[1,2,32]{2,1,0:T(2,128)S(1)} %maximum_bitcast_fusion.1), channel_id=2, replica_groups=mesh['seq_0'=8,'seq_1'=2,'exp_0'=4,'exp_1'=8] {'seq_0'}, dimensions={0}, use_global_device_ids=true | all-gather | bytes 2304 | tf_op jit(solution)/shard_map/all_gather | solution.py:54
  39.8 7.0 %all-gather.5 = f32[2,2,32]{2,1,0:T(2,128)S(1)} all-gather(f32[1,2,32]{2,1,0:T(2,128)S(1)} %maximum_bitcast_fusion.2), channel_id=3, replica_groups=mesh['seq_0'=8,'seq_1'=2,'exp_0'=4,'exp_1'=8] {'seq_1'}, dimensions={0}, use_global_device_ids=true | all-gather | bytes 768 | tf_op jit(solution)/shard_map/all_gather | solution.py:54
  46.8 6.1 %all-gather.6 = f32[4,2,32]{2,1,0:T(2,128)S(1)} all-gather(f32[1,2,32]{2,1,0:T(2,128)S(1)} %maximum_bitcast_fusion.3), channel_id=4, replica_groups=mesh['seq_0'=8,'seq_1'=2,'exp_0'=4,'exp_1'=8] {'exp_0'}, dimensions={0}, use_global_device_ids=true | all-gather | bytes 1280 | tf_op jit(solution)/shard_map/all_gather | solution.py:54
  53.0 10.5 %all-gather.7 = f32[8,2,32]{2,1,0:T(2,128)S(1)} all-gather(f32[1,2,32]{2,1,0:T(2,128)S(1)} %maximum_bitcast_fusion.4), channel_id=5, replica_groups=mesh['seq_0'=8,'seq_1'=2,'exp_0'=4,'exp_1'=8] {'exp_1'}, dimensions={0}, use_global_device_ids=true | all-gather | bytes 2304 | tf_op jit(solution)/shard_map/all_gather | solution.py:54
  63.5 0.2 fusion.26
  64.0 0.3 copy.17
  64.3 14.2 %all_to_all.46 = f32[32,1,2560]{2,1,0:T(1,128)S(1)} all-to-all(f32[32,1,2560]{2,1,0:T(1,128)S(1)} %copy.17), channel_id=1, replica_groups=mesh['seq_0'=8,'seq_1'=2,'exp_0'=4,'exp_1'=8] {'exp_0','exp_1'}, dimensions={0} | all-to-all | bytes 655360 | tf_op jit(solution)/shard_map/all_to_all | solution.py:23
  78.8 21.2 %all_to_all.47 = f32[16,1,2560]{2,1,0:T(1,128)S(1)} all-to-all(f32[16,1,2560]{2,1,0:T(1,128)S(1)} %broadcast_in_dim.15), channel_id=1, replica_groups=mesh['seq_0'=8,'seq_1'=2,'exp_0'=4,'exp_1'=8] {'seq_0','seq_1'}, dimensions={0} | all-to-all | bytes 327680 | tf_op jit(solution)/shard_map/all_to_all | solution.py:29
  100.2 0.3 convolution_reduce_fusion.2
  100.5 0.3 convolution_reduce_fusion.3
  100.9 0.2 convolution_reduce_fusion
  101.2 0.7 broadcast_in_dim.36
  101.8 3.4 %all-to-all-start.5 = ((f32[16,1,1280]{2,1,0:T(1,128)}), f32[16,1,1280]{2,1,0:T(1,128)S(1)}, u32[]{:S(2)}, u32[]{:S(2)}) async-start(f32[16,1,1280]{2,1,0:T(1,128)} %broadcast_in_dim.36), calls=%async_computation.5 | async-start | bytes 163840 | tf_op jit(solution)/shard_map/all_to_all | solution.py:29
  105.3 0.2 convolution_reduce_fusion.1
  105.5 7.4 %all-to-all-done.5 = f32[16,1,1280]{2,1,0:T(1,128)S(1)} async-done(((f32[16,1,1280]{2,1,0:T(1,128)}), f32[16,1,1280]{2,1,0:T(1,128)S(1)}, u32[]{:S(2)}, u32[]{:S(2)}) %all-to-all-start.5) | async-done | bytes 81952 | tf_op jit(solution)/shard_map/all_to_all | solution.py:29
  112.9 0.7 broadcast_in_dim.16
  113.6 3.4 %all-to-all-start.3 = ((f32[16,1,1280]{2,1,0:T(1,128)}), f32[16,1,1280]{2,1,0:T(1,128)S(1)}, u32[]{:S(2)}, u32[]{:S(2)}) async-start(f32[16,1,1280]{2,1,0:T(1,128)} %broadcast_in_dim.16), calls=%async_computation.3 | async-start | bytes 163840 | tf_op jit(solution)/shard_map/all_to_all | solution.py:29
  117.3 1.1 reduce.21
  118.4 0.7 reshape.1145
  119.0 6.2 %all-to-all-done.3 = f32[16,1,1280]{2,1,0:T(1,128)S(1)} async-done(((f32[16,1,1280]{2,1,0:T(1,128)}), f32[16,1,1280]{2,1,0:T(1,128)S(1)}, u32[]{:S(2)}, u32[]{:S(2)}) %all-to-all-start.3) | async-done | bytes 81952 | tf_op jit(solution)/shard_map/all_to_all | solution.py:29
  125.2 4.8 %all-to-all-start.6 = ((bf16[32,2,640]{2,1,0:T(2,128)(2,1)}), bf16[32,2,640]{2,1,0:T(2,128)(2,1)S(1)}, u32[]{:S(2)}, u32[]{:S(2)}) async-start(bf16[32,2,640]{2,1,0:T(2,128)(2,1)} %reshape.1145), calls=%async_computation.6 | async-start | bytes 163840 | tf_op jit(solution)/shard_map/all_to_all | solution.py:29
  130.0 1.4 multiply_convert_fusion
  131.6 1.1 reduce.20
  132.7 0.7 reshape.1143
  133.3 5.6 %all-to-all-done.6 = bf16[32,2,640]{2,1,0:T(2,128)(2,1)S(1)} async-done(((bf16[32,2,640]{2,1,0:T(2,128)(2,1)}), bf16[32,2,640]{2,1,0:T(2,128)(2,1)S(1)}, u32[]{:S(2)}, u32[]{:S(2)}) %all-to-all-start.6) | async-done | bytes 81952 | tf_op jit(solution)/shard_map/all_to_all | solution.py:29
  138.9 3.9 %all-to-all-start.4 = ((bf16[32,2,640]{2,1,0:T(2,128)(2,1)}), bf16[32,2,640]{2,1,0:T(2,128)(2,1)S(1)}, u32[]{:S(2)}, u32[]{:S(2)}) async-start(bf16[32,2,640]{2,1,0:T(2,128)(2,1)} %reshape.1143), calls=%async_computation.4 | async-start | bytes 163840 | tf_op jit(solution)/shard_map/all_to_all | solution.py:29
  143.0 8.8 %all-to-all-done.4 = bf16[32,2,640]{2,1,0:T(2,128)(2,1)S(1)} async-done(((bf16[32,2,640]{2,1,0:T(2,128)(2,1)}), bf16[32,2,640]{2,1,0:T(2,128)(2,1)S(1)}, u32[]{:S(2)}, u32[]{:S(2)}) %all-to-all-start.4) | async-done | bytes 81952 | tf_op jit(solution)/shard_map/all_to_all | solution.py:29
  151.9 0.2 multiply_reduce_fusion.1
  152.1 10.9 %psum.28 = f32[32]{0:T(128)S(1)} all-reduce(f32[32]{0:T(128)S(1)} %get-tuple-element.6), channel_id=1, replica_groups=mesh['seq_0'=8,'seq_1'=2,'exp_0'=4,'exp_1'=8] {'seq_0'}, use_global_device_ids=true, to_apply=%region_10.11 | all-reduce | flops 32 | bytes 256 | tf_op jit(solution)/shard_map/psum | solution.py:74
  163.0 8.6 %psum.29 = f32[32]{0:T(128)S(1)} all-reduce(f32[32]{0:T(128)S(1)} %psum.28), channel_id=1, replica_groups=mesh['seq_0'=8,'seq_1'=2,'exp_0'=4,'exp_1'=8] {'seq_1'}, use_global_device_ids=true, to_apply=%region_11.12 | all-reduce | flops 32 | bytes 256 | tf_op jit(solution)/shard_map/psum | solution.py:74
  171.6 6.8 %psum.30 = f32[32]{0:T(128)S(1)} all-reduce(f32[32]{0:T(128)S(1)} %psum.29), channel_id=1, replica_groups=mesh['seq_0'=8,'seq_1'=2,'exp_0'=4,'exp_1'=8] {'exp_0'}, use_global_device_ids=true, to_apply=%region_12.13 | all-reduce | flops 32 | bytes 256 | tf_op jit(solution)/shard_map/psum | solution.py:74
  178.4 11.3 %psum.31 = f32[32]{0:T(128)S(1)} all-reduce(f32[32]{0:T(128)S(1)} %psum.30), channel_id=1, replica_groups=mesh['seq_0'=8,'seq_1'=2,'exp_0'=4,'exp_1'=8] {'exp_1'}, use_global_device_ids=true, to_apply=%region_13.14 | all-reduce | flops 32 | bytes 256 | tf_op jit(solution)/shard_map/psum | solution.py:74
  189.7 0.2 convolution_bitcast_fusion
  189.9 0.8 copy.21
  190.8 4.4 %all-to-all-start.7 = ((f32[32,1,1280]{2,1,0:T(1,128)}), f32[32,1,1280]{2,1,0:T(1,128)S(1)}, u32[]{:S(2)}, u32[]{:S(2)}) async-start(f32[32,1,1280]{2,1,0:T(1,128)} %copy.21), calls=%async_computation.7 | async-start | bytes 327680 | tf_op jit(solution)/shard_map/all_to_all | solution.py:23
  195.1 0.3 fusion.7
  195.5 1.1 fusion
  196.6 7.8 %all-to-all-done.7 = f32[32,1,1280]{2,1,0:T(1,128)S(1)} async-done(((f32[32,1,1280]{2,1,0:T(1,128)}), f32[32,1,1280]{2,1,0:T(1,128)S(1)}, u32[]{:S(2)}, u32[]{:S(2)}) %all-to-all-start.7) | async-done | bytes 163872 | tf_op jit(solution)/shard_map/all_to_all | solution.py:23
  204.5 0.7 broadcast_in_dim.38
  205.2 11.8 %all-to-all-start.8 = ((f32[16,1,1280]{2,1,0:T(1,128)}), f32[16,1,1280]{2,1,0:T(1,128)S(1)}, u32[]{:S(2)}, u32[]{:S(2)}) async-start(f32[16,1,1280]{2,1,0:T(1,128)} %broadcast_in_dim.38), calls=%async_computation.8 | async-start | bytes 163840 | tf_op jit(solution)/shard_map/all_to_all | solution.py:29
  217.0 1.0 convolution_convert_fusion
  218.0 7.1 %all-to-all-done.8 = f32[16,1,1280]{2,1,0:T(1,128)S(1)} async-done(((f32[16,1,1280]{2,1,0:T(1,128)}), f32[16,1,1280]{2,1,0:T(1,128)S(1)}, u32[]{:S(2)}, u32[]{:S(2)}) %all-to-all-start.8) | async-done | bytes 81952 | tf_op jit(solution)/shard_map/all_to_all | solution.py:29
  225.2 0.6 transpose.20
  (41 shorter events, 2.0 us)
Async XLA Ops:
  0.6 99.9 %copy-start = (bf16[1,320,1280]{2,1,0:T(8,128)(2,1)S(1)}, bf16[1,320,1280]{2,1,0:T(8,128)(2,1)}, u32[]{:S(2)}) copy-start(bf16[1,320,1280]{2,1,0:T(8,128)(2,1)} %param.7) | copy-start | bytes 2457604
  0.6 25.2 %copy-start.1 = (bf16[128,1280]{1,0:T(8,128)(2,1)S(1)}, bf16[128,1280]{1,0:T(8,128)(2,1)}, u32[]{:S(2)}) copy-start(bf16[128,1280]{1,0:T(8,128)(2,1)} %param.5) | copy-start | bytes 983044
  3.2 60.6 %copy-start.3 = (bf16[128,1280]{1,0:T(8,128)(2,1)S(1)}, bf16[128,1280]{1,0:T(8,128)(2,1)}, u32[]{:S(2)}) copy-start(bf16[128,1280]{1,0:T(8,128)(2,1)} %param.9) | copy-start | bytes 983044
  64.3 35.9 %copy-start.2 = (bf16[1,320,1280]{2,1,0:T(8,128)(2,1)S(1)}, bf16[1,320,1280]{2,1,0:T(8,128)(2,1)}, u32[]{:S(2)}) copy-start(bf16[1,320,1280]{2,1,0:T(8,128)(2,1)} %param.8) | copy-start | bytes 2457604
  101.8 11.1 %all-to-all-start.5 = ((f32[16,1,1280]{2,1,0:T(1,128)}), f32[16,1,1280]{2,1,0:T(1,128)S(1)}, u32[]{:S(2)}, u32[]{:S(2)}) async-start(f32[16,1,1280]{2,1,0:T(1,128)} %broadcast_in_dim.36), calls=%async_computation.5 | async-start | bytes 163840 | tf_op jit(solution)/shard_map/all_to_all | solution.py:29
  113.6 11.6 %all-to-all-start.3 = ((f32[16,1,1280]{2,1,0:T(1,128)}), f32[16,1,1280]{2,1,0:T(1,128)S(1)}, u32[]{:S(2)}, u32[]{:S(2)}) async-start(f32[16,1,1280]{2,1,0:T(1,128)} %broadcast_in_dim.16), calls=%async_computation.3 | async-start | bytes 163840 | tf_op jit(solution)/shard_map/all_to_all | solution.py:29
  125.2 13.8 %all-to-all-start.6 = ((bf16[32,2,640]{2,1,0:T(2,128)(2,1)}), bf16[32,2,640]{2,1,0:T(2,128)(2,1)S(1)}, u32[]{:S(2)}, u32[]{:S(2)}) async-start(bf16[32,2,640]{2,1,0:T(2,128)(2,1)} %reshape.1145), calls=%async_computation.6 | async-start | bytes 163840 | tf_op jit(solution)/shard_map/all_to_all | solution.py:29
  138.9 12.9 %all-to-all-start.4 = ((bf16[32,2,640]{2,1,0:T(2,128)(2,1)}), bf16[32,2,640]{2,1,0:T(2,128)(2,1)S(1)}, u32[]{:S(2)}, u32[]{:S(2)}) async-start(bf16[32,2,640]{2,1,0:T(2,128)(2,1)} %reshape.1143), calls=%async_computation.4 | async-start | bytes 163840 | tf_op jit(solution)/shard_map/all_to_all | solution.py:29
  190.8 13.6 %all-to-all-start.7 = ((f32[32,1,1280]{2,1,0:T(1,128)}), f32[32,1,1280]{2,1,0:T(1,128)S(1)}, u32[]{:S(2)}, u32[]{:S(2)}) async-start(f32[32,1,1280]{2,1,0:T(1,128)} %copy.21), calls=%async_computation.7 | async-start | bytes 327680 | tf_op jit(solution)/shard_map/all_to_all | solution.py:23
  205.2 19.9 %all-to-all-start.8 = ((f32[16,1,1280]{2,1,0:T(1,128)}), f32[16,1,1280]{2,1,0:T(1,128)S(1)}, u32[]{:S(2)}, u32[]{:S(2)}) async-start(f32[16,1,1280]{2,1,0:T(1,128)} %broadcast_in_dim.38), calls=%async_computation.8 | async-start | bytes 163840 | tf_op jit(solution)/shard_map/all_to_all | solution.py:29
where the time goes:
time: 227 us; the launch traced here: 226 us
  blocking collectives  133 us (59%)
  waiting for transfers between devices  42.9 us (19%)
  starting transfers between devices  31.7 us (14%)
  other arithmetic  6.5 us (3%)
  local copies, waits for them, and re-layouts  6.29 us (3%)
  matrix products  4.99 us (2%)
    all_to_all x2, blocking collectives, sent_to_all(): return lax.all_to_all(copies, axis, split_axis=0, concat_axis=0, tiled=True)  43.8 us
    psum x4, blocking collectives, by_axis(): value = lax.psum(value, axis)  37.6 us
    all_gather x4, blocking collectives, collected_together(): both, at, found = (lax.all_gather(jnp.concatenate(lines), axis), 0, {})  37 us
    all_to_all x5, waiting for transfers between devices, sent_to_all(): return lax.all_to_all(copies, axis, split_axis=0, concat_axis=0, tiled=True)  35.1 us
    all_to_all x5, starting transfers between devices, sent_to_all(): return lax.all_to_all(copies, axis, split_axis=0, concat_axis=0, tiled=True)  27.3 us
    all_to_all x1, blocking collectives, sent_and_summed(): lax.all_to_all(tiles, axis, split_axis=0, concat_axis=0, tiled=True)  14.2 us
    all_to_all x1, waiting for transfers between devices, sent_and_summed(): lax.all_to_all(tiles, axis, split_axis=0, concat_axis=0, tiled=True)  7.81 us
  transfers between devices with their start and end apart: 6, of which 6 were waited for; matrix products, arithmetic and copies ran while one was open for 4% of the time, Pallas kernels for 0%

commit v1 on v0

v1 whole, which is shorter than its diff:
```python
import functools

import jax
import jax.numpy as jnp
from jax import lax
from jax.experimental import pallas as pl
from jax.experimental.pallas import tpu as pltpu
from jax.sharding import PartitionSpec as P

tanh_coeff = 0.7978845608028654
cubic_coeff = 0.044715
F32 = jnp.float32
BF16 = jnp.bfloat16
MESH = pl.DeviceIdType.MESH
LANES = 128


def gelu_value(values):
    return (
        0.5
        * values
        * (1.0 + jnp.tanh(tanh_coeff * (values + cubic_coeff * values * values * values)))
    )


def gelu_slope(values):
    tanh_part = jnp.tanh(tanh_coeff * (values + cubic_coeff * values * values * values))
    return 0.5 * (1.0 + tanh_part) + 0.5 * values * (1.0 - tanh_part * tanh_part) * tanh_coeff * (
        1.0 + 3.0 * cubic_coeff * values * values
    )


def split_in_three(value):
    high = value.astype(BF16).astype(F32)
    rest = value - high
    middle = rest.astype(BF16).astype(F32)
    return high, middle, rest - middle


def packed_scalars(values):
    rows = values[0].shape[0]
    lane = lax.broadcasted_iota(jnp.int32, (rows, LANES), 1)
    result = jnp.zeros((rows, LANES), F32)
    at = 0
    for value in values:
        for part in split_in_three(value):
            result = jnp.where(lane == at, part, result)
            at += 1
    return result


def unpacked_scalars(row, count):
    lane = lax.broadcasted_iota(jnp.int32, row.shape, 1)
    found = []
    for k in range(count):
        mine = (lane >= 3 * k) & (lane < 3 * k + 3)
        found.append(jnp.sum(jnp.where(mine, row, 0.0), axis=1, keepdims=True))
    return found


def high_and_low(value):
    high = value.astype(BF16).astype(F32)
    return high, value - high


def pair_of_rows(row):
    high, low = high_and_low(row)
    at = lax.broadcasted_iota(jnp.int32, (16, 1), 0)
    return jnp.where(at == 0, high, jnp.where(at == 1, low, 0.0)).astype(BF16)


def dot(a, b, dims):
    return lax.dot_general(a, b, (dims, ((), ())), preferred_element_type=F32)


def kernel(
    n_seq, n_exp, x_hbm, keys_hbm, w_in_hbm, w_out_hbm, c_hbm,
    layer_out, tokens_grad, keys_grad, w_in_grad, w_out_grad,
    x, keys_ref, c, w_in, w_out, k_all, so, sg, row_f, flat_f,
    a_buf, c1_send_in, c1_send_grad, c1_in, c1_grad, c2_in, c2_grad,
    e_out, e_grad, f_buf, h1_send, h1_buf, h2_buf,
    load_sem, send_sem, recv_sem,
):
    width = x.shape[1]
    blocks = width // LANES
    pairs = blocks // 2
    tall = blocks + 1
    s_me = lax.axis_index("seq")
    e_me = lax.axis_index("exp")

    loads = [
        pltpu.make_async_copy(source, target, load_sem.at[k])
        for k, (source, target) in enumerate(
            ((x_hbm, x), (c_hbm, c), (w_in_hbm, w_in), (w_out_hbm, w_out), (keys_hbm, keys_ref))
        )
    ]

    barrier = pltpu.get_barrier_semaphore()

    def greet_exp(k, carry):
        pl.semaphore_signal(
            barrier, inc=1, device_id=(s_me, lax.rem(e_me + k, n_exp)), device_id_type=MESH
        )
        return carry

    def greet_seq(k, carry):
        pl.semaphore_signal(
            barrier, inc=1, device_id=(lax.rem(s_me + k, n_seq), e_me), device_id_type=MESH
        )
        return carry

    loads[4].start()
    lax.fori_loop(1, n_exp, greet_exp, 0)
    lax.fori_loop(1, n_seq, greet_seq, 0)
    for load in loads[:4]:
        load.start()

    def exchange(over_exp, *parts):
        n, me = (n_exp, e_me) if over_exp else (n_seq, s_me)

        def send(k, carry):
            peer = lax.rem(me + k, n)
            target = (s_me, peer) if over_exp else (peer, e_me)
            for at, unit, source, buf in parts:
                mine = buf.at[pl.ds(me * unit, unit)]
                pltpu.make_async_remote_copy(
                    src_ref=mine if source is None else source.at[pl.ds(peer * unit, unit)],
                    dst_ref=mine,
                    send_sem=send_sem.at[at],
                    recv_sem=recv_sem.at[at],
                    device_id=target,
                    device_id_type=MESH,
                ).start()
            return carry

        lax.fori_loop(1, n, send, 0)

    def whole(over_exp, at, unit, source, buf):
        n, me = (n_exp, e_me) if over_exp else (n_seq, s_me)
        peer = lax.rem(me + 1, n)
        every = buf.at[pl.ds(0, (n - 1) * unit)]
        return pltpu.make_async_remote_copy(
            src_ref=every,
            dst_ref=every,
            send_sem=send_sem.at[at],
            recv_sem=recv_sem.at[at],
            device_id=(s_me, peer) if over_exp else (peer, e_me),
            device_id_type=MESH,
        )

    started = []

    def begin(over_exp, *parts):
        exchange(over_exp, *parts)
        started.extend(whole(over_exp, *part) for part in parts)

        def arrived():
            for part in parts:
                whole(over_exp, *part).wait_recv()

        return arrived

    def cut(row):
        return [row[:, k * LANES : (k + 1) * LANES] for k in range(blocks)]

    def store_pairs(buf, me, rows):
        for k, row in enumerate(rows):
            row_f[pl.ds(k, 1), :] = row
        count = len(rows)
        unit = count // 2
        buf[pl.ds(me * unit, unit)] = row_f[0:count, :].reshape(unit, 2, LANES).astype(BF16)

    def store_rows(buf, me, unit, rows):
        for k, row in enumerate(rows):
            buf[pl.ds(me * unit + k, 1)] = row.reshape(1, 1, LANES)

    def load_pairs(buf):
        count = buf.shape[0] * 2
        flat_f[0:count, :] = buf.reshape(count, LANES)[...].astype(F32)

    def picked(source, row, count, rows):
        return source[pl.ds(row, count, stride=rows), :]

    def split_to(target, first, rows, values):
        for k in range(blocks):
            target[pl.ds(first + k, n_exp, stride=rows), :] = values[:, k * LANES : (k + 1) * LANES]

    lane = lax.broadcasted_iota(jnp.int32, (1, LANES), 1)

    def two_scalars(a, b):
        return jnp.where(lane < LANES // 2, a, b)

    loads[4].wait()
    store_pairs(a_buf, e_me, cut(keys_ref[...].astype(F32)))
    pl.semaphore_wait(barrier, n_exp - 1 + n_seq - 1)
    arrived = begin(True, (0, pairs, None, a_buf))
    loads[0].wait()
    loads[1].wait()
    arrived()
    load_pairs(a_buf)
    for k in range(blocks):
        k_all[:, k * LANES : (k + 1) * LANES] = picked(flat_f, k, n_exp, blocks).astype(BF16)

    logits = dot(k_all[...], x[...], ((1,), (1,)))
    local_peak = jnp.max(logits, axis=1, keepdims=True)
    local_terms = jnp.exp(logits - local_peak)
    local_total = jnp.sum(local_terms, axis=1, keepdims=True)
    row_peak = jnp.max(logits, axis=0, keepdims=True)
    row_terms = jnp.exp(logits - row_peak)
    comb_prob = row_terms / jnp.sum(row_terms, axis=0, keepdims=True)
    combine = comb_prob.astype(BF16)

    def rows_of(weights, data):
        both = jnp.concatenate(high_and_low(weights), axis=0).astype(BF16)
        result = dot(both, data[...], ((1,), (0,)))
        return result[0:n_exp] + result[n_exp:]

    grad_view = c1_send_grad.reshape(n_exp * tall, LANES)
    grad_view[pl.ds(blocks, n_exp, stride=tall), :] = two_scalars(local_peak, local_total)
    split_to(grad_view, 0, tall, rows_of(comb_prob, c))
    split_to(flat_f, 0, blocks, rows_of(local_terms, x))
    c1_send_in.reshape(n_exp * blocks, LANES)[...] = flat_f[0 : n_exp * blocks, :].astype(BF16)
    c1_grad[pl.ds(e_me * tall, tall)] = c1_send_grad[pl.ds(e_me * tall, tall)]
    c1_in[pl.ds(e_me * pairs, pairs)] = c1_send_in[pl.ds(e_me * pairs, pairs)]
    arrived = begin(True, (1, tall, c1_send_grad, c1_grad), (2, pairs, c1_send_in, c1_in))
    arrived()

    def summed(source, count, rows, scale=None):
        result = []
        for k in range(blocks):
            part = picked(source, k, count, rows)
            if scale is not None:
                part = part * scale
            result.append(jnp.sum(part, axis=0, keepdims=True))
        return result

    def merged(buf_in, buf_grad, count):
        grad = buf_grad.reshape(count * tall, LANES)
        load_pairs(buf_in)
        stats = picked(grad, blocks, count, tall)
        peaks, totals = stats[:, 0:1], stats[:, LANES // 2 : LANES // 2 + 1]
        peak = jnp.max(peaks, axis=0, keepdims=True)
        scale = jnp.exp(peaks - peak)
        total = jnp.sum(scale * totals, axis=0, keepdims=True)
        return summed(flat_f, count, blocks, scale), summed(grad, count, tall), peak, total

    first, second, peak, total = merged(c1_in, c1_grad, n_exp)
    store_rows(c2_grad, s_me, tall, second + [two_scalars(peak, total)])
    store_pairs(c2_in, s_me, first)
    arrived = begin(False, (3, tall, None, c2_grad), (4, pairs, None, c2_in))
    loads[2].wait()
    loads[3].wait()
    arrived()
    first, second, slot_peak, slot_total = merged(c2_in, c2_grad, n_seq)
    slot_in = [part / slot_total for part in first]

    def times(row, matrix, dim):
        result = dot(row, matrix[...], ((1,), (dim,)))
        return result[0:1] + result[1:2]

    in_lhs = pair_of_rows(jnp.concatenate(slot_in, axis=1))
    out_lhs = pair_of_rows(jnp.concatenate(second, axis=1))
    pre_act = times(in_lhs, w_in, 1)
    act_grad = times(out_lhs, w_out, 1)
    activation = gelu_value(pre_act)
    pre_grad = act_grad * gelu_slope(pre_act)
    slot_out_part = times(pair_of_rows(activation), w_out, 0)
    slot_in_grad_part = times(pair_of_rows(pre_grad), w_in, 0)

    store_rows(e_grad, s_me, blocks, cut(slot_in_grad_part))
    store_pairs(e_out, s_me, cut(slot_out_part))
    arrived = begin(False, (5, blocks, None, e_grad), (6, pairs, None, e_out))

    first_row = lax.broadcasted_iota(jnp.int32, (16, 1), 0) == 0
    act_lhs = jnp.where(first_row, activation, 0.0).astype(BF16)
    pre_lhs = jnp.where(first_row, pre_grad, 0.0).astype(BF16)
    step = 2 * LANES
    for k in range(width // step):
        cols = slice(k * step, (k + 1) * step)
        w_out_grad[:, cols] = dot(act_lhs, out_lhs[:, cols], ((0,), (0,))).astype(BF16)
        w_in_grad[:, cols] = dot(pre_lhs, in_lhs[:, cols], ((0,), (0,))).astype(BF16)

    arrived()
    slot_in_grad = summed(e_grad.reshape(n_seq * blocks, LANES), n_seq, blocks)
    load_pairs(e_out)
    slot_out = summed(flat_f, n_seq, blocks)
    products = [a * b.astype(BF16).astype(F32) for a, b in zip(slot_in, slot_in_grad)]
    correction = jnp.sum(functools.reduce(jnp.add, products), axis=1, keepdims=True)

    both = 2 * (blocks + 1)
    scalars = packed_scalars((slot_peak, slot_total, correction))
    store_pairs(f_buf, e_me, slot_out + slot_in_grad + [scalars, jnp.zeros((1, LANES), F32)])
    arrived = begin(True, (7, both // 2, None, f_buf))
    arrived()
    load_pairs(f_buf)
    for k in range(blocks):
        cols = slice(k * LANES, (k + 1) * LANES)
        so[:, cols] = picked(flat_f, k, n_exp, both).astype(BF16)
        sg[:, cols] = picked(flat_f, blocks + k, n_exp, both).astype(BF16)
    peaks, totals, corrections = unpacked_scalars(picked(flat_f, 2 * blocks, n_exp, both), 3)

    comb_grad = dot(so[...], c[...], ((1,), (1,)))
    disp_grad = dot(sg[...], x[...], ((1,), (1,)))
    disp_prob = jnp.exp(logits - peaks) / totals
    comb_mean = jnp.sum(comb_prob * comb_grad, axis=0, keepdims=True)
    logit_grad = (
        comb_prob * (comb_grad - comb_mean) + disp_prob * (disp_grad - corrections)
    ).astype(BF16)

    split_to(flat_f, 0, blocks, dot(logit_grad, x[...], ((1,), (0,))))
    h1_send.reshape(n_exp * blocks, LANES)[...] = flat_f[0 : n_exp * blocks, :].astype(BF16)
    h1_buf[pl.ds(e_me * pairs, pairs)] = h1_send[pl.ds(e_me * pairs, pairs)]
    arrived = begin(True, (8, pairs, h1_send, h1_buf))

    layer_out[...] = dot(combine, so[...], ((0,), (0,))).astype(BF16)
    tokens_grad[...] = (
        dot(disp_prob.astype(BF16), sg[...], ((0,), (0,))) + dot(logit_grad, k_all[...], ((0,), (0,)))
    ).astype(BF16)

    arrived()
    load_pairs(h1_buf)
    store_pairs(h2_buf, s_me, summed(flat_f, n_exp, blocks))

    arrived = begin(False, (9, pairs, None, h2_buf))
    for copies in started:
        copies.wait_send()
    arrived()
    load_pairs(h2_buf)
    for k, part in enumerate(summed(flat_f, n_seq, blocks)):
        keys_grad[:, k * LANES : (k + 1) * LANES] = part


def put_kernel(*refs):
    count = (len(refs) - 1) // 2
    copies = [
        pltpu.make_async_copy(refs[k], refs[count + k], refs[-1].at[k]) for k in range(count)
    ]
    for copy in copies:
        copy.start()
    for copy in copies:
        copy.wait()


def put(arrays):
    count = len(arrays)
    return pl.pallas_call(
        put_kernel,
        out_shape=tuple(pltpu.HBM(a.shape, a.dtype) for a in arrays),
        in_specs=[pl.BlockSpec(memory_space=pltpu.VMEM)] * count,
        out_specs=(pl.BlockSpec(memory_space=pltpu.HBM),) * count,
        scratch_shapes=[pltpu.SemaphoreType.DMA((count,))],
        compiler_params=pltpu.CompilerParams(vmem_limit_bytes=1024 * 1024),
        name="put",
    )(*arrays)


def local(n_seq, n_exp, tokens, slot_keys, w_in, w_out, cotangent):
    rows, width = tokens.shape
    hidden = w_in.shape[1]
    blocks = width // LANES
    pairs = blocks // 2
    tall = blocks + 1

    def pairs_of(count):
        return pltpu.VMEM((count, 2, LANES), BF16)

    def rows_of(count):
        return pltpu.VMEM((count, 1, LANES), F32)

    hbm = pl.BlockSpec(memory_space=pltpu.HBM)
    vmem = pl.BlockSpec(memory_space=pltpu.VMEM)
    layer_out, tokens_grad, keys_grad, w_in_grad, w_out_grad = pl.pallas_call(
        functools.partial(kernel, n_seq, n_exp),
        out_shape=(
            pltpu.VMEM((rows, width), BF16),
            pltpu.VMEM((rows, width), BF16),
            pltpu.VMEM((1, width), F32),
            pltpu.VMEM((hidden, width), BF16),
            pltpu.VMEM((hidden, width), BF16),
        ),
        in_specs=[hbm, hbm, hbm, hbm, hbm],
        out_specs=(vmem, vmem, vmem, vmem, vmem),
        scratch_shapes=[
            pltpu.VMEM((rows, width), BF16),
            pltpu.VMEM((1, width), BF16),
            pltpu.VMEM((rows, width), BF16),
            pltpu.VMEM((hidden, width), BF16),
            pltpu.VMEM((hidden, width), BF16),
            pltpu.VMEM((n_exp, width), BF16),
            pltpu.VMEM((n_exp, width), BF16),
            pltpu.VMEM((n_exp, width), BF16),
            pltpu.VMEM((2 * tall, LANES), F32),
            pltpu.VMEM((max(n_seq, n_exp) * 2 * tall, LANES), F32),
            pairs_of(n_exp * pairs),
            pairs_of(n_exp * pairs),
            rows_of(n_exp * tall),
            pairs_of(n_exp * pairs),
            rows_of(n_exp * tall),
            pairs_of(n_seq * pairs),
            rows_of(n_seq * tall),
            pairs_of(n_seq * pairs),
            rows_of(n_seq * blocks),
            pairs_of(n_exp * tall),
            pairs_of(n_exp * pairs),
            pairs_of(n_exp * pairs),
            pairs_of(n_seq * pairs),
            pltpu.SemaphoreType.DMA((5,)),
            pltpu.SemaphoreType.DMA((10,)),
            pltpu.SemaphoreType.DMA((10,)),
        ],
        compiler_params=pltpu.CompilerParams(
            collective_id=0, has_side_effects=True, vmem_limit_bytes=32 * 1024 * 1024
        ),
        name="moe",
    )(
        *(
            pltpu.with_memory_space_constraint(a, pltpu.HBM)
            for a in (tokens, slot_keys.T, w_in[0], w_out[0], cotangent)
        )
    )
    layer_out, tokens_grad, keys_grad, w_in_grad, w_out_grad = put(
        (layer_out, tokens_grad, keys_grad, w_in_grad, w_out_grad)
    )
    return layer_out, tokens_grad, keys_grad.T, w_in_grad[None], w_out_grad[None]


def solution(mesh):
    n_seq, n_exp = mesh.shape["seq"], mesh.shape["exp"]
    placed = (
        P(("seq", "exp"), None),
        P(None, "exp"),
        P("exp", "seq", None),
        P("exp", "seq", None),
        P(("seq", "exp"), None),
    )
    return jax.shard_map(
        functools.partial(local, n_seq, n_exp),
        mesh=mesh,
        in_specs=placed,
        out_specs=(
            P(("seq", "exp"), None),
            P(("seq", "exp"), None),
            P(None, "exp"),
            P("exp", "seq", None),
            P("exp", "seq", None),
        ),
        check_vma=False,
    )
```

time: 227 us -> 67.8 us (0.30)
  blocking collectives: 133 us -> 0 us
  Pallas kernels: 0 us -> 67 us
  waiting for transfers between devices: 42.9 us -> 0 us
  starting transfers between devices: 31.7 us -> 0 us
  other arithmetic: 6.5 us -> 0 us
  local copies, waits for them, and re-layouts: 6.29 us -> 0 us
  matrix products: 4.99 us -> 0 us
    pallas_call x0 -> x2, Pallas kernels: none -> 67 us  [the longest x1 65.6 us: local(): pl.pallas_call(functools.partial(kernel, n_seq, n_exp), out_shape=(pltpu....]
    all_to_all x3 -> x0, blocking collectives: 58 us -> none  [the longest x2 43.8 us: sent_to_all(): return lax.all_to_all(copies, axis, split_axis=0, concat_axis=0, tiled=True)]
    all_to_all x6 -> x0, waiting for transfers between devices: 42.9 us -> none  [the longest x5 35.1 us: sent_to_all(): return lax.all_to_all(copies, axis, split_axis=0, concat_axis=0, tiled=True)]
    psum x4 -> x0, blocking collectives: 37.6 us -> none  [by_axis(): value = lax.psum(value, axis)]
    all_gather x4 -> x0, blocking collectives: 37 us -> none  [collected_together(): both, at, found = (lax.all_gather(jnp.concatenate(lines), axis), 0, {})]
    all_to_all x6 -> x0, starting transfers between devices: 31.7 us -> none  [the longest x5 27.3 us: sent_to_all(): return lax.all_to_all(copies, axis, split_axis=0, concat_axis=0, tiled=True)]
    dot_general x13 -> x0, matrix products: 4.99 us -> none  [the longest x1 1.09 us: local(): lax.dot_general(logit_grad, keys_all, (((0,), (1,)), ((), ())), preferred...]
    broadcast_in_dim x6 -> x0, local copies, waits for them, and re-layouts: 2.29 us -> none  [sent_to_all(): copies = jnp.broadcast_to(value, (lax.axis_size(axis), *value.shape))]
  transfers between devices with their start and end apart: 6 -> 0, of which waited for: 6 -> 0; matrix products, arithmetic and copies ran while one was open for 4% -> 0% of each run, Pallas kernels for 0% -> 0%
where the time goes in v1:
time: 67.8 us; the launch traced here: 67.6 us
  Pallas kernels  67 us (99%)
    pallas_call x1, Pallas kernels, local(): pl.pallas_call(functools.partial(kernel, n_seq, n_exp), out_shape=(pltpu....  65.6 us
    pallas_call x1, Pallas kernels, put(): pl.pallas_call(put_kernel, out_shape=tuple((pltpu.HBM(a.shape, a.dtype) f...  1.43 us

profile of v1, /device:TPU:1, one launch (start us, length us, event | category | flops | bytes accessed | tf_op | source)
XLA Modules:
  0.0 67.6 jit_solution(3355799205049485400)
XLA Ops:
  0.6 65.6 %moe.1 = (bf16[128,1280]{1,0:T(8,128)(2,1)S(1)}, bf16[128,1280]{1,0:T(8,128)(2,1)S(1)}, f32[1,1280]{1,0:T(1,128)S(1)}, bf16[320,1280]{1,0:T(8,128)(2,1)S(1)}, bf16[320,1280]{1,0:T(8,128)(2,1)S(1)}) custom-call(bf16[128,1280]{1,0:T(8,128)(2,1)} %x_hbm.1, bf16[1,1280]{1,0:T(2,128)(2,1)} %bitcast.8, bf16[320,1280]{1,0:T(8,128)(2,1)} %bitcast.6, ...), custom_call_target="tpu_custom_call" | custom-call | tf_op jit(solution)/shard_map/moe/pallas_call | solution.py:372
  66.2 1.4 %put.1 = (bf16[128,1280]{1,0:T(8,128)(2,1)}, bf16[128,1280]{1,0:T(8,128)(2,1)}, f32[1,1280]{1,0:T(1,128)}, bf16[320,1280]{1,0:T(8,128)(2,1)}, bf16[320,1280]{1,0:T(8,128)(2,1)}) custom-call(bf16[128,1280]{1,0:T(8,128)(2,1)S(1)} %get-tuple-element.15.refs_0_, bf16[128,1280]{1,0:T(8,128)(2,1)S(1)} %get-tuple-element.16.refs_1_, ...), custom_call_target="tpu_custom_call" | custom-call | tf_op jit(solution)/shard_map/put/pallas_call | solution.py:346

commit v2 on v1

--- a/solution.py
+++ b/solution.py
@@ -71,6 +71,16 @@
 
 def dot(a, b, dims):
     return lax.dot_general(a, b, (dims, ((), ())), preferred_element_type=F32)
+
+
+def farthest_first(n, over_exp):
+    inner = 8 if over_exp and n % 8 == 0 else n
+
+    def hops(k):
+        near, far = k % inner, k // inner
+        return min(near, inner - near) + min(far, n // inner - far)
+
+    return sorted(range(1, n), key=lambda k: -hops(k))
 
 
 def kernel(
@@ -118,7 +128,7 @@
     def exchange(over_exp, *parts):
         n, me = (n_exp, e_me) if over_exp else (n_seq, s_me)
 
-        def send(k, carry):
+        for k in farthest_first(n, over_exp):
             peer = lax.rem(me + k, n)
             target = (s_me, peer) if over_exp else (peer, e_me)
             for at, unit, source, buf in parts:
@@ -131,9 +141,6 @@
                     device_id=target,
                     device_id_type=MESH,
                 ).start()
-            return carry
-
-        lax.fori_loop(1, n, send, 0)
 
     def whole(over_exp, at, unit, source, buf):
         n, me = (n_exp, e_me) if over_exp else (n_seq, s_me)
@@ -218,11 +225,13 @@
     grad_view = c1_send_grad.reshape(n_exp * tall, LANES)
     grad_view[pl.ds(blocks, n_exp, stride=tall), :] = two_scalars(local_peak, local_total)
     split_to(grad_view, 0, tall, rows_of(comb_prob, c))
+    c1_grad[pl.ds(e_me * tall, tall)] = c1_send_grad[pl.ds(e_me * tall, tall)]
+    arrived_grad = begin(True, (1, tall, c1_send_grad, c1_grad))
     split_to(flat_f, 0, blocks, rows_of(local_terms, x))
     c1_send_in.reshape(n_exp * blocks, LANES)[...] = flat_f[0 : n_exp * blocks, :].astype(BF16)
-    c1_grad[pl.ds(e_me * tall, tall)] = c1_send_grad[pl.ds(e_me * tall, tall)]
     c1_in[pl.ds(e_me * pairs, pairs)] = c1_send_in[pl.ds(e_me * pairs, pairs)]
-    arrived = begin(True, (1, tall, c1_send_grad, c1_grad), (2, pairs, c1_send_in, c1_in))
+    arrived = begin(True, (2, pairs, c1_send_in, c1_in))
+    arrived_grad()
     arrived()
 
     def summed(source, count, rows, scale=None):
@@ -332,9 +341,17 @@
 
 def put_kernel(*refs):
     count = (len(refs) - 1) // 2
-    copies = [
-        pltpu.make_async_copy(refs[k], refs[count + k], refs[-1].at[k]) for k in range(count)
-    ]
+    copies = []
+    for k in range(count):
+        rows = refs[k].shape[0]
+        parts = 2 if rows % 32 == 0 else 1
+        for part in range(parts):
+            at = pl.ds(part * (rows // parts), rows // parts)
+            copies.append(
+                pltpu.make_async_copy(
+                    refs[k].at[at], refs[count + k].at[at], refs[-1].at[2 * k + part]
+                )
+            )
     for copy in copies:
         copy.start()
     for copy in copies:
@@ -348,7 +365,7 @@
         out_shape=tuple(pltpu.HBM(a.shape, a.dtype) for a in arrays),
         in_specs=[pl.BlockSpec(memory_space=pltpu.VMEM)] * count,
         out_specs=(pl.BlockSpec(memory_space=pltpu.HBM),) * count,
-        scratch_shapes=[pltpu.SemaphoreType.DMA((count,))],
+        scratch_shapes=[pltpu.SemaphoreType.DMA((2 * count,))],
         compiler_params=pltpu.CompilerParams(vmem_limit_bytes=1024 * 1024),
         name="put",
     )(*arrays)

time: 67.8 us -> 64.3 us (0.948)
  Pallas kernels: 67 us -> 63.5 us
    pallas_call x1, Pallas kernels: 65.6 us -> 62 us  [local(): pl.pallas_call(functools.partial(kernel, n_seq, n_exp), out_shape=(pltpu....]
where the time goes in v2:
time: 64.3 us; the launch traced here: 64.2 us
  Pallas kernels  63.5 us (99%)
    pallas_call x1, Pallas kernels, local(): pl.pallas_call(functools.partial(kernel, n_seq, n_exp), out_shape=(pltpu....  62 us
    pallas_call x1, Pallas kernels, put(): pl.pallas_call(put_kernel, out_shape=tuple((pltpu.HBM(a.shape, a.dtype) f...  1.47 us

profile of v2, /device:TPU:1, one launch (start us, length us, event | category | flops | bytes accessed | tf_op | source)
XLA Modules:
  0.0 64.2 jit_solution(18092995954246460119)
XLA Ops:
  0.6 62.0 %moe.1 = (bf16[128,1280]{1,0:T(8,128)(2,1)S(1)}, bf16[128,1280]{1,0:T(8,128)(2,1)S(1)}, f32[1,1280]{1,0:T(1,128)S(1)}, bf16[320,1280]{1,0:T(8,128)(2,1)S(1)}, bf16[320,1280]{1,0:T(8,128)(2,1)S(1)}) custom-call(bf16[128,1280]{1,0:T(8,128)(2,1)} %x_hbm.1, bf16[1,1280]{1,0:T(2,128)(2,1)} %bitcast.8, bf16[320,1280]{1,0:T(8,128)(2,1)} %bitcast.6, ...), custom_call_target="tpu_custom_call" | custom-call | tf_op jit(solution)/shard_map/moe/pallas_call | solution.py:389
  62.7 1.5 %put.1 = (bf16[128,1280]{1,0:T(8,128)(2,1)}, bf16[128,1280]{1,0:T(8,128)(2,1)}, f32[1,1280]{1,0:T(1,128)}, bf16[320,1280]{1,0:T(8,128)(2,1)}, bf16[320,1280]{1,0:T(8,128)(2,1)}) custom-call(bf16[128,1280]{1,0:T(8,128)(2,1)S(1)} %get-tuple-element.15.refs_0_, bf16[128,1280]{1,0:T(8,128)(2,1)S(1)} %get-tuple-element.16.refs_1_, ...), custom_call_target="tpu_custom_call" | custom-call | tf_op jit(solution)/shard_map/put/pallas_call | solution.py:363

commit v3 on v2

--- a/solution.py
+++ b/solution.py
@@ -61,12 +61,6 @@
 def high_and_low(value):
     high = value.astype(BF16).astype(F32)
     return high, value - high
-
-
-def pair_of_rows(row):
-    high, low = high_and_low(row)
-    at = lax.broadcasted_iota(jnp.int32, (16, 1), 0)
-    return jnp.where(at == 0, high, jnp.where(at == 1, low, 0.0)).astype(BF16)
 
 
 def dot(a, b, dims):
@@ -107,21 +101,15 @@
 
     barrier = pltpu.get_barrier_semaphore()
 
-    def greet_exp(k, carry):
+    loads[4].start()
+    for k in farthest_first(n_exp, True):
         pl.semaphore_signal(
             barrier, inc=1, device_id=(s_me, lax.rem(e_me + k, n_exp)), device_id_type=MESH
         )
-        return carry
-
-    def greet_seq(k, carry):
+    for k in farthest_first(n_seq, False):
         pl.semaphore_signal(
             barrier, inc=1, device_id=(lax.rem(s_me + k, n_seq), e_me), device_id_type=MESH
         )
-        return carry
-
-    loads[4].start()
-    lax.fori_loop(1, n_exp, greet_exp, 0)
-    lax.fori_loop(1, n_seq, greet_seq, 0)
     for load in loads[:4]:
         load.start()
 
@@ -217,17 +205,14 @@
     comb_prob = row_terms / jnp.sum(row_terms, axis=0, keepdims=True)
     combine = comb_prob.astype(BF16)
 
-    def rows_of(weights, data):
-        both = jnp.concatenate(high_and_low(weights), axis=0).astype(BF16)
-        result = dot(both, data[...], ((1,), (0,)))
-        return result[0:n_exp] + result[n_exp:]
-
     grad_view = c1_send_grad.reshape(n_exp * tall, LANES)
     grad_view[pl.ds(blocks, n_exp, stride=tall), :] = two_scalars(local_peak, local_total)
-    split_to(grad_view, 0, tall, rows_of(comb_prob, c))
+    split_to(grad_view, 0, tall, dot(combine, c[...], ((1,), (0,))))
     c1_grad[pl.ds(e_me * tall, tall)] = c1_send_grad[pl.ds(e_me * tall, tall)]
     arrived_grad = begin(True, (1, tall, c1_send_grad, c1_grad))
-    split_to(flat_f, 0, blocks, rows_of(local_terms, x))
+    both_terms = jnp.concatenate(high_and_low(local_terms), axis=0).astype(BF16)
+    in_rows = dot(both_terms, x[...], ((1,), (0,)))
+    split_to(flat_f, 0, blocks, in_rows[0:n_exp] + in_rows[n_exp:])
     c1_send_in.reshape(n_exp * blocks, LANES)[...] = flat_f[0 : n_exp * blocks, :].astype(BF16)
     c1_in[pl.ds(e_me * pairs, pairs)] = c1_send_in[pl.ds(e_me * pairs, pairs)]
     arrived = begin(True, (2, pairs, c1_send_in, c1_in))
@@ -263,26 +248,27 @@
     first, second, slot_peak, slot_total = merged(c2_in, c2_grad, n_seq)
     slot_in = [part / slot_total for part in first]
 
+    in_first = lax.broadcasted_iota(jnp.int32, (16, 1), 0) == 0
+
+    def first_row(row):
+        return jnp.where(in_first, row, 0.0).astype(BF16)
+
     def times(row, matrix, dim):
-        result = dot(row, matrix[...], ((1,), (dim,)))
-        return result[0:1] + result[1:2]
-
-    in_lhs = pair_of_rows(jnp.concatenate(slot_in, axis=1))
-    out_lhs = pair_of_rows(jnp.concatenate(second, axis=1))
+        return dot(row, matrix[...], ((1,), (dim,)))[0:1]
+
+    in_lhs = first_row(jnp.concatenate(slot_in, axis=1))
+    out_lhs = first_row(jnp.concatenate(second, axis=1))
     pre_act = times(in_lhs, w_in, 1)
     act_grad = times(out_lhs, w_out, 1)
-    activation = gelu_value(pre_act)
-    pre_grad = act_grad * gelu_slope(pre_act)
-    slot_out_part = times(pair_of_rows(activation), w_out, 0)
-    slot_in_grad_part = times(pair_of_rows(pre_grad), w_in, 0)
+    act_lhs = first_row(gelu_value(pre_act))
+    pre_lhs = first_row(act_grad * gelu_slope(pre_act))
+    slot_in_grad_part = times(pre_lhs, w_in, 0)
+    slot_out_part = times(act_lhs, w_out, 0)
 
     store_rows(e_grad, s_me, blocks, cut(slot_in_grad_part))
     store_pairs(e_out, s_me, cut(slot_out_part))
     arrived = begin(False, (5, blocks, None, e_grad), (6, pairs, None, e_out))
 
-    first_row = lax.broadcasted_iota(jnp.int32, (16, 1), 0) == 0
-    act_lhs = jnp.where(first_row, activation, 0.0).astype(BF16)
-    pre_lhs = jnp.where(first_row, pre_grad, 0.0).astype(BF16)
     step = 2 * LANES
     for k in range(width // step):
         cols = slice(k * step, (k + 1) * step)

time: 64.3 us -> 63.9 us (level)
  no operation moved by 1% of the time
where the time goes in v3:
time: 63.9 us; the launch traced here: 63.8 us
  Pallas kernels  63.1 us (99%)
  between operations  0.64 us (1%)
    pallas_call x1, Pallas kernels, local(): pl.pallas_call(functools.partial(kernel, n_seq, n_exp), out_shape=(pltpu....  61.7 us
    pallas_call x1, Pallas kernels, put(): pl.pallas_call(put_kernel, out_shape=tuple((pltpu.HBM(a.shape, a.dtype) f...  1.47 us

profile of v3, /device:TPU:1, one launch (start us, length us, event | category | flops | bytes accessed | tf_op | source)
XLA Modules:
  0.0 63.8 jit_solution(12600455531338883167)
XLA Ops:
  0.6 61.7 %moe.1 = (bf16[128,1280]{1,0:T(8,128)(2,1)S(1)}, bf16[128,1280]{1,0:T(8,128)(2,1)S(1)}, f32[1,1280]{1,0:T(1,128)S(1)}, bf16[320,1280]{1,0:T(8,128)(2,1)S(1)}, bf16[320,1280]{1,0:T(8,128)(2,1)S(1)}) custom-call(bf16[128,1280]{1,0:T(8,128)(2,1)} %x_hbm.1, bf16[1,1280]{1,0:T(2,128)(2,1)} %bitcast.8, bf16[320,1280]{1,0:T(8,128)(2,1)} %bitcast.6, ...), custom_call_target="tpu_custom_call" | custom-call | tf_op jit(solution)/shard_map/moe/pallas_call | solution.py:375
  62.3 1.5 %put.1 = (bf16[128,1280]{1,0:T(8,128)(2,1)}, bf16[128,1280]{1,0:T(8,128)(2,1)}, f32[1,1280]{1,0:T(1,128)}, bf16[320,1280]{1,0:T(8,128)(2,1)}, bf16[320,1280]{1,0:T(8,128)(2,1)}) custom-call(bf16[128,1280]{1,0:T(8,128)(2,1)S(1)} %get-tuple-element.15.refs_0_, bf16[128,1280]{1,0:T(8,128)(2,1)S(1)} %get-tuple-element.16.refs_1_, ...), custom_call_target="tpu_custom_call" | custom-call | tf_op jit(solution)/shard_map/put/pallas_call | solution.py:349

commit v4 on v3

--- a/solution.py
+++ b/solution.py
@@ -215,9 +215,7 @@
     split_to(flat_f, 0, blocks, in_rows[0:n_exp] + in_rows[n_exp:])
     c1_send_in.reshape(n_exp * blocks, LANES)[...] = flat_f[0 : n_exp * blocks, :].astype(BF16)
     c1_in[pl.ds(e_me * pairs, pairs)] = c1_send_in[pl.ds(e_me * pairs, pairs)]
-    arrived = begin(True, (2, pairs, c1_send_in, c1_in))
-    arrived_grad()
-    arrived()
+    arrived_in = begin(True, (2, pairs, c1_send_in, c1_in))
 
     def summed(source, count, rows, scale=None):
         result = []
@@ -228,25 +226,28 @@
             result.append(jnp.sum(part, axis=0, keepdims=True))
         return result
 
-    def merged(buf_in, buf_grad, count):
-        grad = buf_grad.reshape(count * tall, LANES)
-        load_pairs(buf_in)
+    def merged_grad(buf, count):
+        grad = buf.reshape(count * tall, LANES)
         stats = picked(grad, blocks, count, tall)
         peaks, totals = stats[:, 0:1], stats[:, LANES // 2 : LANES // 2 + 1]
         peak = jnp.max(peaks, axis=0, keepdims=True)
         scale = jnp.exp(peaks - peak)
         total = jnp.sum(scale * totals, axis=0, keepdims=True)
-        return summed(flat_f, count, blocks, scale), summed(grad, count, tall), peak, total
-
-    first, second, peak, total = merged(c1_in, c1_grad, n_exp)
-    store_rows(c2_grad, s_me, tall, second + [two_scalars(peak, total)])
-    store_pairs(c2_in, s_me, first)
-    arrived = begin(False, (3, tall, None, c2_grad), (4, pairs, None, c2_in))
+        return summed(grad, count, tall), peak, total, scale
+
+    def merged_in(buf, count, scale):
+        load_pairs(buf)
+        return summed(flat_f, count, blocks, scale)
+
+    arrived_grad()
+    out_grad, peak, total, scale = merged_grad(c1_grad, n_exp)
+    store_rows(c2_grad, s_me, tall, out_grad + [two_scalars(peak, total)])
+    arrived_grad = begin(False, (3, tall, None, c2_grad))
+    arrived_in()
+    store_pairs(c2_in, s_me, merged_in(c1_in, n_exp, scale))
+    arrived_in = begin(False, (4, pairs, None, c2_in))
     loads[2].wait()
     loads[3].wait()
-    arrived()
-    first, second, slot_peak, slot_total = merged(c2_in, c2_grad, n_seq)
-    slot_in = [part / slot_total for part in first]
 
     in_first = lax.broadcasted_iota(jnp.int32, (16, 1), 0) == 0
 
@@ -256,10 +257,14 @@
     def times(row, matrix, dim):
         return dot(row, matrix[...], ((1,), (dim,)))[0:1]
 
+    arrived_grad()
+    out_grad, slot_peak, slot_total, scale = merged_grad(c2_grad, n_seq)
+    out_lhs = first_row(jnp.concatenate(out_grad, axis=1))
+    act_grad = times(out_lhs, w_out, 1)
+    arrived_in()
+    slot_in = [part / slot_total for part in merged_in(c2_in, n_seq, scale)]
     in_lhs = first_row(jnp.concatenate(slot_in, axis=1))
-    out_lhs = first_row(jnp.concatenate(second, axis=1))
     pre_act = times(in_lhs, w_in, 1)
-    act_grad = times(out_lhs, w_out, 1)
     act_lhs = first_row(gelu_value(pre_act))
     pre_lhs = first_row(act_grad * gelu_slope(pre_act))
     slot_in_grad_part = times(pre_lhs, w_in, 0)

time: 63.9 us -> 63.7 us (level)
  no operation moved by 1% of the time
where the time goes in v4:
time: 63.7 us; the launch traced here: 63.5 us
  Pallas kernels  62.9 us (99%)
  between operations  0.64 us (1%)
    pallas_call x1, Pallas kernels, local(): pl.pallas_call(functools.partial(kernel, n_seq, n_exp), out_shape=(pltpu....  61.4 us
    pallas_call x1, Pallas kernels, put(): pl.pallas_call(put_kernel, out_shape=tuple((pltpu.HBM(a.shape, a.dtype) f...  1.47 us

profile of v4, /device:TPU:1, one launch (start us, length us, event | category | flops | bytes accessed | tf_op | source)
XLA Modules:
  0.0 63.5 jit_solution(15760552839233931014)
XLA Ops:
  0.6 61.4 %moe.1 = (bf16[128,1280]{1,0:T(8,128)(2,1)S(1)}, bf16[128,1280]{1,0:T(8,128)(2,1)S(1)}, f32[1,1280]{1,0:T(1,128)S(1)}, bf16[320,1280]{1,0:T(8,128)(2,1)S(1)}, bf16[320,1280]{1,0:T(8,128)(2,1)S(1)}) custom-call(bf16[128,1280]{1,0:T(8,128)(2,1)} %x_hbm.1, bf16[1,1280]{1,0:T(2,128)(2,1)} %bitcast.8, bf16[320,1280]{1,0:T(8,128)(2,1)} %bitcast.6, ...), custom_call_target="tpu_custom_call" | custom-call | tf_op jit(solution)/shard_map/moe/pallas_call | solution.py:380
  62.0 1.5 %put.1 = (bf16[128,1280]{1,0:T(8,128)(2,1)}, bf16[128,1280]{1,0:T(8,128)(2,1)}, f32[1,1280]{1,0:T(1,128)}, bf16[320,1280]{1,0:T(8,128)(2,1)}, bf16[320,1280]{1,0:T(8,128)(2,1)}) custom-call(bf16[128,1280]{1,0:T(8,128)(2,1)S(1)} %get-tuple-element.15.refs_0_, bf16[128,1280]{1,0:T(8,128)(2,1)S(1)} %get-tuple-element.16.refs_1_, ...), custom_call_target="tpu_custom_call" | custom-call | tf_op jit(solution)/shard_map/put/pallas_call | solution.py:354

commit v5 on v4

--- a/solution.py
+++ b/solution.py
@@ -56,11 +56,6 @@
         mine = (lane >= 3 * k) & (lane < 3 * k + 3)
         found.append(jnp.sum(jnp.where(mine, row, 0.0), axis=1, keepdims=True))
     return found
-
-
-def high_and_low(value):
-    high = value.astype(BF16).astype(F32)
-    return high, value - high
 
 
 def dot(a, b, dims):
@@ -210,9 +205,7 @@
     split_to(grad_view, 0, tall, dot(combine, c[...], ((1,), (0,))))
     c1_grad[pl.ds(e_me * tall, tall)] = c1_send_grad[pl.ds(e_me * tall, tall)]
     arrived_grad = begin(True, (1, tall, c1_send_grad, c1_grad))
-    both_terms = jnp.concatenate(high_and_low(local_terms), axis=0).astype(BF16)
-    in_rows = dot(both_terms, x[...], ((1,), (0,)))
-    split_to(flat_f, 0, blocks, in_rows[0:n_exp] + in_rows[n_exp:])
+    split_to(flat_f, 0, blocks, dot(local_terms.astype(BF16), x[...], ((1,), (0,))))
     c1_send_in.reshape(n_exp * blocks, LANES)[...] = flat_f[0 : n_exp * blocks, :].astype(BF16)
     c1_in[pl.ds(e_me * pairs, pairs)] = c1_send_in[pl.ds(e_me * pairs, pairs)]
     arrived_in = begin(True, (2, pairs, c1_send_in, c1_in))
@@ -332,17 +325,9 @@
 
 def put_kernel(*refs):
     count = (len(refs) - 1) // 2
-    copies = []
-    for k in range(count):
-        rows = refs[k].shape[0]
-        parts = 2 if rows % 32 == 0 else 1
-        for part in range(parts):
-            at = pl.ds(part * (rows // parts), rows // parts)
-            copies.append(
-                pltpu.make_async_copy(
-                    refs[k].at[at], refs[count + k].at[at], refs[-1].at[2 * k + part]
-                )
-            )
+    copies = [
+        pltpu.make_async_copy(refs[k], refs[count + k], refs[-1].at[k]) for k in range(count)
+    ]
     for copy in copies:
         copy.start()
     for copy in copies:
@@ -356,7 +341,7 @@
         out_shape=tuple(pltpu.HBM(a.shape, a.dtype) for a in arrays),
         in_specs=[pl.BlockSpec(memory_space=pltpu.VMEM)] * count,
         out_specs=(pl.BlockSpec(memory_space=pltpu.HBM),) * count,
-        scratch_shapes=[pltpu.SemaphoreType.DMA((2 * count,))],
+        scratch_shapes=[pltpu.SemaphoreType.DMA((count,))],
         compiler_params=pltpu.CompilerParams(vmem_limit_bytes=1024 * 1024),
         name="put",
     )(*arrays)

time: 63.7 us -> 63.6 us (level)
  no operation moved by 1% of the time
where the time goes in v5:
time: 63.6 us; the launch traced here: 63.5 us
  Pallas kernels  62.8 us (99%)
  between operations  0.64 us (1%)
    pallas_call x1, Pallas kernels, local(): pl.pallas_call(functools.partial(kernel, n_seq, n_exp), out_shape=(pltpu....  61.4 us
    pallas_call x1, Pallas kernels, put(): pl.pallas_call(put_kernel, out_shape=tuple((pltpu.HBM(a.shape, a.dtype) f...  1.43 us

profile of v5, /device:TPU:1, one launch (start us, length us, event | category | flops | bytes accessed | tf_op | source)
XLA Modules:
  0.0 63.5 jit_solution(13545914551684163884)
XLA Ops:
  0.6 61.4 %moe.1 = (bf16[128,1280]{1,0:T(8,128)(2,1)S(1)}, bf16[128,1280]{1,0:T(8,128)(2,1)S(1)}, f32[1,1280]{1,0:T(1,128)S(1)}, bf16[320,1280]{1,0:T(8,128)(2,1)S(1)}, bf16[320,1280]{1,0:T(8,128)(2,1)S(1)}) custom-call(bf16[128,1280]{1,0:T(8,128)(2,1)} %x_hbm.1, bf16[1,1280]{1,0:T(2,128)(2,1)} %bitcast.8, bf16[320,1280]{1,0:T(8,128)(2,1)} %bitcast.6, ...), custom_call_target="tpu_custom_call" | custom-call | tf_op jit(solution)/shard_map/moe/pallas_call | solution.py:365
  62.0 1.4 %put.1 = (bf16[128,1280]{1,0:T(8,128)(2,1)}, bf16[128,1280]{1,0:T(8,128)(2,1)}, f32[1,1280]{1,0:T(1,128)}, bf16[320,1280]{1,0:T(8,128)(2,1)}, bf16[320,1280]{1,0:T(8,128)(2,1)}) custom-call(bf16[128,1280]{1,0:T(8,128)(2,1)S(1)} %get-tuple-element.15.refs_0_, bf16[128,1280]{1,0:T(8,128)(2,1)S(1)} %get-tuple-element.16.refs_1_, ...), custom_call_target="tpu_custom_call" | custom-call | tf_op jit(solution)/shard_map/put/pallas_call | solution.py:339
